TPU v7x, 32 devices: a whole 2x2x4 slice. The times are simulated.
32 devices in a mesh: rep: 2 (over y), span: 2 (over core), seq: 4 (over z), tp: 2 (over x).
Axes of the slice: x: 2, y: 2, z: 4, core: 2. Of those that a mesh axis runs over, the one named last changes fastest.
Arguments:
- queries: bfloat16 [8, 512, 24, 128], P(('rep', 'span'), 'seq', 'tp'), parts along dimension 0, may hold values from -110 to 110
- key_states: bfloat16 [8, 512, 4, 128], P(('rep', 'span'), 'seq', 'tp'), parts along dimension 0, may hold values from -11 to 11
- value_states: bfloat16 [8, 512, 4, 128], P(('rep', 'span'), 'seq', 'tp'), parts along dimension 0, may hold values from -6 to 6
- out_weight: bfloat16 [3072, 6144], P('tp', 'seq'), may hold values from -0.109375 to 0.109375
- noise_table: float32 [64, 6144], P(None, 'tp'), may hold values from 0.5 to 2
- plan: int32 [8], P('rep'), parts along dimension 0, may hold values from 0 to 63
Outputs:
- branch_out: bfloat16 [8, 512, 6144], P(('rep', 'span'), 'seq', 'tp'), parts along dimension 0
There are 2 independent parts, one for each index of `rep`. A program takes and returns all parts, laid end to end along the dimension named above; an argument that names none is the same for every part. Nothing has to cross between parts.
All inputs are finite; a program needn't handle non-finite values.
Results may differ from a plain program's by a relative error of at most 0.014.
Values may be sent and summed in bfloat16 or wider, within the bound.
A program may use at most 128 MiB of HBM per device.

v0:
```python
import jax
import jax.numpy as jnp
from jax import lax
from jax.sharding import PartitionSpec as P


def fold_block(carried, query_rows, key_rows, value_rows, factor):
    maxima, totals, weighted = carried
    scores = (
        jnp.einsum("tkgd,skd->tkgs", query_rows, key_rows, preferred_element_type=jnp.float32)
        * factor
    )
    highest = jnp.maximum(maxima, jnp.max(scores, axis=-1))
    shrink = jnp.exp(maxima - highest)
    weights = jnp.exp(scores - highest[..., None])
    totals = totals * shrink + jnp.sum(weights, axis=-1)
    weighted = weighted * shrink[..., None] + jnp.einsum(
        "tkgs,skd->tkgd",
        weights.astype(jnp.bfloat16),
        value_rows,
        preferred_element_type=jnp.float32,
    )
    return (maxima * 0.0 + highest, totals, weighted)


def per_device(queries, key_states, value_states, out_weight, noise_table, plan):
    ch_dev, tok_dev, heads_local, head_size = queries.shape
    kv_local = key_states.shape[2]
    per_kv = heads_local // kv_local
    span_count = ch_dev * lax.axis_size("span")
    first_span = lax.axis_index("span") * ch_dev
    factor = head_size ** (-0.5)
    grouped = queries.reshape(ch_dev, tok_dev, kv_local, per_kv, head_size)
    start_max = jnp.full((ch_dev, tok_dev, kv_local, per_kv), -1e30, jnp.float32)
    start_tot = jnp.zeros((ch_dev, tok_dev, kv_local, per_kv), jnp.float32)
    start_acc = jnp.zeros((ch_dev, tok_dev, kv_local, per_kv, head_size), jnp.float32)
    span_rows = (
        lax.all_gather(key_states, "seq", axis=1, tiled=True),
        lax.all_gather(value_states, "seq", axis=1, tiled=True),
    )
    key_piece = lax.all_gather(span_rows[0], "span", axis=0, tiled=True)
    value_piece = lax.all_gather(span_rows[1], "span", axis=0, tiled=True)
    new_max = []
    new_tot = []
    new_acc = []
    for q_span in range(ch_dev):
        inner_state = (start_max[q_span], start_tot[q_span], start_acc[q_span])
        for k_span in range(span_count):

            def update(inner, q_span=q_span, k_span=k_span):
                return fold_block(
                    inner, grouped[q_span], key_piece[k_span], value_piece[k_span], factor
                )

            inner_state = lax.cond(
                k_span <= first_span + q_span, update, lambda inner: inner, inner_state
            )
        new_max.append(inner_state[0])
        new_tot.append(inner_state[1])
        new_acc.append(inner_state[2])
    attn = (
        (jnp.stack(new_acc) / jnp.stack(new_tot)[..., None])
        .reshape(ch_dev, tok_dev, heads_local * head_size)
        .astype(jnp.bfloat16)
    )
    columns = jnp.einsum(
        "ctf,fo->cto",
        lax.all_gather(attn, "seq", axis=1, tiled=True),
        out_weight,
        preferred_element_type=jnp.float32,
    )
    partial_out = lax.all_to_all(
        columns.astype(jnp.bfloat16), "seq", split_axis=1, concat_axis=2, tiled=True
    ).astype(columns.dtype)
    summed = lax.psum_scatter(
        partial_out.astype(jnp.bfloat16), "tp", scatter_dimension=2, tiled=True
    ).astype(jnp.float32)
    levels = lax.dynamic_slice_in_dim(plan, first_span, ch_dev)
    picks = (levels[:, None] == jnp.arange(noise_table.shape[0], dtype=jnp.int32)[None, :]).astype(
        jnp.float32
    )
    gates = jnp.dot(picks, noise_table, precision=lax.Precision.HIGHEST)
    return (summed * gates[:, None, :]).astype(jnp.bfloat16)


def solution(mesh):
    placed = (
        P(("rep", "span"), "seq", "tp", None),
        P(("rep", "span"), "seq", "tp", None),
        P(("rep", "span"), "seq", "tp", None),
        P("tp", "seq"),
        P(None, "tp"),
        P("rep"),
    )
    return jax.shard_map(
        per_device,
        mesh=mesh,
        in_specs=placed,
        out_specs=P(("rep", "span"), "seq", "tp"),
        check_vma=False,
    )
```

profile of v0, /device:TPU:0, one launch (start us, length us, event | category | flops | bytes accessed | tf_op | source)
XLA Modules:
  0.0 320.5 jit_solution(18199733619609409647)
XLA Ops:
  7.5 18.0 %all_gather.15 = bf16[2,512,2,128]{3,1,2,0:T(8,128)(2,1)} all-gather(bf16[2,128,2,128]{3,1,2,0:T(8,128)(2,1)S(1)} %copy.63), channel_id=1, replica_groups=mesh['rep'=2,'span'=2,'seq'=4,'tp'=2] {'seq'}, dimensions={1}, use_global_device_ids=true | all-gather | bytes 655360 | tf_op jit(solution)/shard_map/all_gather | solution.py:38
  26.5 17.0 %all_gather.17 = bf16[2,512,2,128]{3,1,2,0:T(8,128)(2,1)} all-gather(bf16[2,128,2,128]{3,1,2,0:T(8,128)(2,1)S(1)} %copy.64), channel_id=1, replica_groups=mesh['rep'=2,'span'=2,'seq'=4,'tp'=2] {'seq'}, dimensions={1}, use_global_device_ids=true | all-gather | bytes 655360 | tf_op jit(solution)/shard_map/all_gather | solution.py:39
  43.7 9.6 %all-gather.6.cloned.1.call-done = bf16[4,512,2,128]{3,1,2,0:T(8,128)(2,1)} async-done(((bf16[2,512,2,128]{3,1,2,0:T(8,128)(2,1)}), bf16[4,512,2,128]{3,1,2,0:T(8,128)(2,1)}) %all-gather.6.cloned.1.call-update) | async-done | bytes 1048592 | tf_op jit(solution)/shard_map/all_gather | solution.py:42
  53.3 6.1 %conditional.12 = (f32[128,2,6]{0,2,1:T(8,128)}, f32[128,2,6]{0,2,1:T(8,128)S(1)}, f32[128,2,6,128]{3,0,2,1:T(8,128)S(1)}) conditional(s32[]{:T(128)} %convert_element_type.70, () %tuple.93, (bf16[4,512,2,128]{3,1,2,0:T(8,128)(2,1)}, bf16[2,128,2,6,128]{4,1,3,2,0:T(8,128)(2,1)}, bf16[4,512,2,128]{3,1,2,0:T(8,128)(2,1)}) %tuple.190), branch_computations={%region_16.0_spmd, %region_17.0_spmd} | conditional | flops 409147392 | bytes 11210776 | solution.py:55
  53.3 1.7 bitcast_reduce_fusion.4
  57.5 1.9 fusion.93
  59.4 6.2 %conditional.13 = ((f32[128,2,6]{0,2,1:T(8,128)}, f32[128,2,6]{0,2,1:T(8,128)S(1)}, f32[128,2,6,128]{3,0,2,1:T(8,128)S(1)})) conditional(s32[]{:T(128)} %convert_element_type.69, (f32[128,2,6]{0,2,1:T(8,128)}, f32[128,2,6]{0,2,1:T(8,128)S(1)}, f32[128,2,6,128]{3,0,2,1:T(8,128)S(1)}) %conditional.12, (f32[128,2,6]{0,2,1:T(8,128)}, ...), branch_computations={%region_20.0_spmd, %region_21.0_spmd} | conditional | flops 409344000 | bytes 12032032 | solution.py:55
  59.4 1.7 bitcast_reduce_fusion.5
  63.6 2.0 fusion.115
  65.6 6.1 %conditional.8 = (f32[128,2,6]{0,2,1:T(8,128)}, f32[128,2,6]{0,2,1:T(8,128)S(1)}, f32[128,2,6,128]{3,0,2,1:T(8,128)S(1)}) conditional(s32[]{:T(128)} %convert_element_type.66, () %tuple.87, (bf16[4,512,2,128]{3,1,2,0:T(8,128)(2,1)}, bf16[2,128,2,6,128]{4,1,3,2,0:T(8,128)(2,1)}, bf16[4,512,2,128]{3,1,2,0:T(8,128)(2,1)}) %tuple.193), branch_computations={%region_0.0_spmd, %region_1.0_spmd} | conditional | flops 409147392 | bytes 11210776 | solution.py:55
  65.6 1.7 bitcast_reduce_fusion
  69.8 1.9 fusion.10
  72.0 1.5 conditional.15
  73.4 1.4 conditional.11
  75.0 1.6 copy.73
  76.6 2.9 fusion.171
  79.6 93.0 %all-gather.8.cloned.1.call-done = bf16[2,512,1536]{2,1,0:T(8,128)(2,1)} async-done(((bf16[2,128,1536]{2,1,0:T(8,128)(2,1)}), bf16[2,512,1536]{2,1,0:T(8,128)(2,1)}) %all-gather.8.cloned.1.call-update) | async-done | bytes 3145744 | tf_op jit(solution)/shard_map/all_gather | solution.py:68
  172.6 8.1 %fusion.168 = bf16[2,512,1536]{2,1,0:T(8,128)(2,1)S(1)} fusion(bf16[2,512,1536]{2,1,0:T(8,128)(2,1)} %all-gather.8.cloned.1.call-done, bf16[1536,1536]{1,0:T(8,128)(2,1)} %param.25), kind=kOutput, calls=%fused_computation.166 | convolution fusion | flops 4833411072 | bytes 11010048 | tf_op jit(solution)/shard_map/ctf,fo->cto/dot_general | solution.py:66
  180.7 3.2 %copy.74 = bf16[2,512,1536]{2,0,1:T(2,128)(2,1)S(1)} copy(bf16[2,512,1536]{2,1,0:T(8,128)(2,1)S(1)} %fusion.168) | data formatting | bytes 6291456 | tf_op jit(solution)/shard_map/convert_element_type | solution.py:73
  183.9 73.3 %all_to_all.18 = bf16[2,512,1536]{2,0,1:T(2,128)(2,1)S(1)} all-to-all(bf16[2,512,1536]{2,0,1:T(2,128)(2,1)S(1)} %copy.74), channel_id=1, replica_groups=mesh['rep'=2,'span'=2,'seq'=4,'tp'=2] {'seq'}, dimensions={1} | all-to-all | bytes 6291456 | tf_op jit(solution)/shard_map/all_to_all | solution.py:72
  257.2 4.1 %copy.75 = bf16[2,128,4,1536]{3,2,1,0:T(4,128)(2,1)} copy(bf16[2,128,4,1536]{3,0,1,2:T(2,128)(2,1)S(1)} %bitcast.326) | data formatting | bytes 6291456 | tf_op jit(solution)/shard_map/all_to_all | solution.py:72
  261.3 6.9 %all_to_all.16 = bf16[2,128,6144]{2,1,0:T(8,128)(2,1)} reshape(bf16[2,128,4,1536]{3,2,1,0:T(4,128)(2,1)} %copy.75) | data formatting | bytes 6291456 | tf_op jit(solution)/shard_map/all_to_all | solution.py:72
  269.4 41.7 %reduce-scatter.2.cloned.1.call-done = bf16[2,128,3072]{2,1,0:T(8,128)(2,1)} async-done(((bf16[2,128,6144]{2,1,0:T(8,128)(2,1)}), bf16[2,128,3072]{2,1,0:T(8,128)(2,1)}) %reduce-scatter.2.cloned.1.call-update) | async-done | bytes 1572880 | tf_op jit(solution)/shard_map/reduce_scatter | solution.py:75
  311.1 2.9 multiply_convert_fusion
  (36 shorter events, 14.0 us)
Async XLA Ops:
  6.5 262.4 %copy-start = (f32[64,3072]{1,0:T(8,128)S(1)}, f32[64,3072]{1,0:T(8,128)}, u32[]{:S(2)}) copy-start(f32[64,3072]{1,0:T(8,128)} %param.26) | copy-start | bytes 2359300
  6.5 37.2 %all-gather.4.cloned.1.call-start = ((), (), s32[]{:S(2)}) async-start(), calls=%async_computation.2 | async-start | bytes 1572864 | tf_op jit(solution)/shard_map/all_gather | solution.py:41
  25.6 27.7 %all-gather.6.cloned.1.call-start = ((), (), s32[]{:S(2)}) async-start(), calls=%async_computation.3 | async-start | bytes 1572864 | tf_op jit(solution)/shard_map/all_gather | solution.py:42
  43.6 129.0 %all-gather.8.cloned.1.call-start = ((), (), s32[]{:S(2)}) async-start(), calls=%async_computation.4 | async-start | bytes 3932160 | tf_op jit(solution)/shard_map/all_gather | solution.py:68
  79.6 231.5 %reduce-scatter.2.cloned.1.call-start = ((), (), s32[]{:S(2)}) async-start(), calls=%async_computation.5 | async-start | bytes 4718592 | tf_op jit(solution)/shard_map/reduce_scatter | solution.py:75
  268.3 0.7 copy-start.5
Sparse Core Ops, SparseCore 0:
  25.7 10.8 all-gather.3
  43.7 9.5 all-gather.5
  79.7 92.8 all-gather.7
  268.4 42.6 reduce-scatter.1
where the time goes:
time: 322 us; the launch traced here: 321 us
  waiting for transfers between devices  144 us (45%)
  blocking collectives  108 us (34%)
  local copies, waits for them, and re-layouts  22.1 us (7%)
  matrix products  19.2 us (6%)
  between operations  13.2 us (4%)
  other arithmetic  12.9 us (4%)
    all_gather x1, waiting for transfers between devices, per_device(): lax.all_gather(attn, 'seq', axis=1, tiled=True)  93 us
    all_to_all x1, blocking collectives, per_device(): lax.all_to_all(columns.astype(jnp.bfloat16), 'seq', split_axis=1, concat_...  73.3 us
    reduce_scatter x1, waiting for transfers between devices, per_device(): lax.psum_scatter(partial_out.astype(jnp.bfloat16), 'tp', scatter_dimensio...  41.7 us
    all_gather x1, blocking collectives, per_device(): lax.all_gather(key_states, 'seq', axis=1, tiled=True)  18 us
    all_gather x1, blocking collectives, per_device(): lax.all_gather(value_states, 'seq', axis=1, tiled=True)  17 us
    all_to_all x2, local copies, waits for them, and re-layouts, per_device(): lax.all_to_all(columns.astype(jnp.bfloat16), 'seq', split_axis=1, concat_...  11 us
    all_gather x1, waiting for transfers between devices, per_device(): value_piece = lax.all_gather(span_rows[1], 'span', axis=0, tiled=True)  9.6 us
    dot_general x1, matrix products, per_device(): jnp.einsum('ctf,fo->cto', lax.all_gather(attn, 'seq', axis=1, tiled=True)...  8.06 us
  transfers between devices with their start and end apart: 4, of which 3 were waited for; matrix products, arithmetic and copies ran while one was open for 0% of the time, Pallas kernels for 0%

commit v1 on v0

--- a/solution.py
+++ b/solution.py
@@ -2,6 +2,25 @@
 import jax.numpy as jnp
 from jax import lax
 from jax.sharding import PartitionSpec as P
+
+
+def in_order(tiles, dim):
+    tiles = jnp.moveaxis(tiles, 0, dim)
+    dims = tiles.shape
+    return tiles.reshape(*dims[:dim], dims[dim] * dims[dim + 1], *dims[dim + 2 :])
+
+
+def ring_apply(x, axis, dim, work, out_dim):
+    size, index, width = (lax.axis_size(axis), lax.axis_index(axis), x.shape[dim])
+    upward = [(i, (i + 1) % size) for i in range(size)]
+    blocks = []
+    carried = x
+    for step in range(size):
+        following = carried if step == size - 1 else lax.ppermute(carried, axis, upward)
+        blocks.append(work(carried, (index - step) % size * width))
+        carried = following
+    blocks = jnp.stack(blocks)[(index - jnp.arange(size)) % size]
+    return in_order(blocks, out_dim)
 
 
 def fold_block(carried, query_rows, key_rows, value_rows, factor):
@@ -63,11 +82,14 @@
         .reshape(ch_dev, tok_dev, heads_local * head_size)
         .astype(jnp.bfloat16)
     )
-    columns = jnp.einsum(
-        "ctf,fo->cto",
-        lax.all_gather(attn, "seq", axis=1, tiled=True),
-        out_weight,
-        preferred_element_type=jnp.float32,
+    columns = ring_apply(
+        attn,
+        "seq",
+        1,
+        lambda own_block, start: jnp.einsum(
+            "ctf,fo->cto", own_block, out_weight, preferred_element_type=jnp.float32
+        ),
+        1,
     )
     partial_out = lax.all_to_all(
         columns.astype(jnp.bfloat16), "seq", split_axis=1, concat_axis=2, tiled=True

time: 322 us -> 281 us (0.87)
  waiting for transfers between devices: 144 us -> 96 us
  local copies, waits for them, and re-layouts: 22.1 us -> 26 us
  matrix products: 19.2 us -> 22.6 us
    all_gather x1 -> x0, waiting for transfers between devices: 93 us -> none  [per_device(): lax.all_gather(attn, 'seq', axis=1, tiled=True)]
    ppermute x0 -> x3, waiting for transfers between devices: none -> 38 us  [ring_apply(): lax.ppermute(carried, axis, upward)]
    reduce_scatter x1, waiting for transfers between devices: 41.7 us -> 48.3 us  [per_device(): lax.psum_scatter(partial_out.astype(jnp.bfloat16), 'tp', scatter_dimensio...]
    gather x0 -> x1, local copies, waits for them, and re-layouts: none -> 4.32 us  [ring_apply(): blocks = jnp.stack(blocks)[(index - jnp.arange(size)) % size]]
    all_to_all x2, local copies, waits for them, and re-layouts: 11 us -> 6.8 us  [per_device(): lax.all_to_all(columns.astype(jnp.bfloat16), 'seq', split_axis=1, concat_...]
    dot_general x1 -> x4, matrix products: 8.06 us -> 11.5 us  [per_device(): jnp.einsum('ctf,fo->cto', own_block, out_weight, preferred_element_type=j...]
  transfers between devices with their start and end apart: 4 -> 6, of which waited for: 3 -> 5; matrix products, arithmetic and copies ran while one was open for 0% -> 4% of each run, Pallas kernels for 0% -> 0%
where the time goes in v1:
time: 281 us; the launch traced here: 280 us
  blocking collectives  107 us (38%)
  waiting for transfers between devices  96 us (34%)
  local copies, waits for them, and re-layouts  26 us (9%)
  matrix products  22.6 us (8%)
  between operations  13.3 us (5%)
  other arithmetic  13.1 us (5%)
    all_to_all x1, blocking collectives, per_device(): lax.all_to_all(columns.astype(jnp.bfloat16), 'seq', split_axis=1, concat_...  72 us
    reduce_scatter x1, waiting for transfers between devices, per_device(): lax.psum_scatter(partial_out.astype(jnp.bfloat16), 'tp', scatter_dimensio...  48.3 us
    ppermute x3, waiting for transfers between devices, ring_apply(): lax.ppermute(carried, axis, upward)  38 us
    all_gather x1, blocking collectives, per_device(): lax.all_gather(key_states, 'seq', axis=1, tiled=True)  18 us
    all_gather x1, blocking collectives, per_device(): lax.all_gather(value_states, 'seq', axis=1, tiled=True)  17 us
    dot_general x4, matrix products, per_device(): jnp.einsum('ctf,fo->cto', own_block, out_weight, preferred_element_type=j...  11.5 us
    all_gather x1, waiting for transfers between devices, per_device(): value_piece = lax.all_gather(span_rows[1], 'span', axis=0, tiled=True)  9.6 us
    all_to_all x2, local copies, waits for them, and re-layouts, per_device(): lax.all_to_all(columns.astype(jnp.bfloat16), 'seq', split_axis=1, concat_...  6.8 us
  transfers between devices with their start and end apart: 6, of which 5 were waited for; matrix products, arithmetic and copies ran while one was open for 4% of the time, Pallas kernels for 0%

profile of v1, /device:TPU:0, one launch (start us, length us, event | category | flops | bytes accessed | tf_op | source)
XLA Modules:
  0.0 280.1 jit_solution(11749001129661108314)
XLA Ops:
  7.5 18.0 %all_gather.12 = bf16[2,512,2,128]{3,1,2,0:T(8,128)(2,1)} all-gather(bf16[2,128,2,128]{3,1,2,0:T(8,128)(2,1)S(1)} %copy.88), channel_id=1, replica_groups=mesh['rep'=2,'span'=2,'seq'=4,'tp'=2] {'seq'}, dimensions={1}, use_global_device_ids=true | all-gather | bytes 655360 | tf_op jit(solution)/shard_map/all_gather | solution.py:57
  26.5 17.0 %all_gather.14 = bf16[2,512,2,128]{3,1,2,0:T(8,128)(2,1)} all-gather(bf16[2,128,2,128]{3,1,2,0:T(8,128)(2,1)S(1)} %copy.89), channel_id=1, replica_groups=mesh['rep'=2,'span'=2,'seq'=4,'tp'=2] {'seq'}, dimensions={1}, use_global_device_ids=true | all-gather | bytes 655360 | tf_op jit(solution)/shard_map/all_gather | solution.py:58
  43.7 9.6 %all-gather.5.cloned.1.call-done = bf16[4,512,2,128]{3,1,2,0:T(8,128)(2,1)} async-done(((bf16[2,512,2,128]{3,1,2,0:T(8,128)(2,1)}), bf16[4,512,2,128]{3,1,2,0:T(8,128)(2,1)}) %all-gather.5.cloned.1.call-update) | async-done | bytes 1048592 | tf_op jit(solution)/shard_map/all_gather | solution.py:61
  53.3 6.1 %conditional.12 = (f32[128,2,6]{0,2,1:T(8,128)}, f32[128,2,6]{0,2,1:T(8,128)S(1)}, f32[128,2,6,128]{3,0,2,1:T(8,128)S(1)}) conditional(s32[]{:T(128)} %convert_element_type.76, () %tuple.93, (bf16[4,512,2,128]{3,1,2,0:T(8,128)(2,1)}, bf16[2,128,2,6,128]{4,1,3,2,0:T(8,128)(2,1)}, bf16[4,512,2,128]{3,1,2,0:T(8,128)(2,1)}) %tuple.198), branch_computations={%region_16.0_spmd, %region_17.0_spmd} | conditional | flops 409147392 | bytes 11210776 | solution.py:74
  57.5 1.9 fusion.93
  59.4 6.2 %conditional.13 = ((f32[128,2,6]{0,2,1:T(8,128)}, f32[128,2,6]{0,2,1:T(8,128)S(1)}, f32[128,2,6,128]{3,0,2,1:T(8,128)S(1)})) conditional(s32[]{:T(128)} %convert_element_type.75, (f32[128,2,6]{0,2,1:T(8,128)}, f32[128,2,6]{0,2,1:T(8,128)S(1)}, f32[128,2,6,128]{3,0,2,1:T(8,128)S(1)}) %conditional.12, (f32[128,2,6]{0,2,1:T(8,128)}, ...), branch_computations={%region_20.0_spmd, %region_21.0_spmd} | conditional | flops 409344000 | bytes 12032032 | solution.py:74
  63.6 2.0 fusion.115
  65.6 6.1 %conditional.8 = (f32[128,2,6]{0,2,1:T(8,128)}, f32[128,2,6]{0,2,1:T(8,128)S(1)}, f32[128,2,6,128]{3,0,2,1:T(8,128)S(1)}) conditional(s32[]{:T(128)} %convert_element_type.72, () %tuple.87, (bf16[4,512,2,128]{3,1,2,0:T(8,128)(2,1)}, bf16[2,128,2,6,128]{4,1,3,2,0:T(8,128)(2,1)}, bf16[4,512,2,128]{3,1,2,0:T(8,128)(2,1)}) %tuple.201), branch_computations={%region_0.0_spmd, %region_1.0_spmd} | conditional | flops 409147392 | bytes 11210776 | solution.py:74
  69.8 1.9 fusion.10
  76.6 2.1 fusion.186
  80.5 12.0 %collective-permute-done = bf16[2,128,1536]{2,1,0:T(8,128)(2,1)S(1)} collective-permute-done((bf16[2,128,1536]{2,1,0:T(8,128)(2,1)S(1)}, bf16[2,128,1536]{2,1,0:T(8,128)(2,1)S(1)}, u32[]{:S(2)}, u32[]{:S(2)}) %collective-permute-start) | collective-permute-done | bytes 786464 | tf_op jit(solution)/shard_map/ppermute | solution.py:19
  92.6 3.9 %fusion.174 = bf16[1,2,128,1536]{3,2,1,0:T(8,128)(2,1)S(1)} fusion(bf16[2,128,1536]{2,1,0:T(8,128)(2,1)S(1)} %fusion.186, bf16[1536,1536]{1,0:T(8,128)(2,1)} %param.25), kind=kOutput, calls=%fused_computation.176 | convolution fusion | flops 1207959552 | bytes 6291456 | tf_op jit(solution)/shard_map/ctf,fo->cto/dot_general | solution.py:89
  96.4 10.0 %collective-permute-done.1 = bf16[2,128,1536]{2,1,0:T(8,128)(2,1)} collective-permute-done((bf16[2,128,1536]{2,1,0:T(8,128)(2,1)S(1)}, bf16[2,128,1536]{2,1,0:T(8,128)(2,1)}, u32[]{:S(2)}, u32[]{:S(2)}) %collective-permute-start.1) | collective-permute-done | bytes 786464 | tf_op jit(solution)/shard_map/ppermute | solution.py:19
  106.4 3.7 %fusion.177 = bf16[1,2,128,1536]{3,2,1,0:T(8,128)(2,1)S(1)} fusion(bf16[2,128,1536]{2,1,0:T(8,128)(2,1)S(1)} %collective-permute-done, bf16[1536,1536]{1,0:T(8,128)(2,1)} %param.25), kind=kOutput, calls=%fused_computation.177 | convolution fusion | flops 1207959552 | bytes 6291456 | tf_op jit(solution)/shard_map/ctf,fo->cto/dot_general | solution.py:89
  110.2 2.5 fusion.180
  112.7 16.0 %collective-permute-done.2 = bf16[2,128,1536]{2,1,0:T(8,128)(2,1)S(1)} collective-permute-done((bf16[2,128,1536]{2,1,0:T(8,128)(2,1)}, bf16[2,128,1536]{2,1,0:T(8,128)(2,1)S(1)}, u32[]{:S(2)}, u32[]{:S(2)}) %collective-permute-start.2) | collective-permute-done | bytes 786464 | tf_op jit(solution)/shard_map/ppermute | solution.py:19
  131.9 4.3 %gather_fusion = bf16[4,2,128,1536]{3,2,1,0:T(8,128)(2,1)} fusion(bf16[4,2,128,1536]{3,2,1,0:T(8,128)(2,1)} %pad_maximum_fusion, s32[1024]{0:T(1024)S(1)} %pad_clamp_fusion), kind=kCustom, calls=%fused_computation | custom fusion | bytes 6291472 | tf_op jit(solution)/shard_map/gather | solution.py:22
  136.2 2.2 copy.99
  138.4 3.2 %copy.100 = bf16[2,512,1536]{2,0,1:T(2,128)(2,1)S(1)} copy(bf16[2,512,1536]{2,1,0:T(8,128)(2,1)S(1)} %bitcast.358) | data formatting | bytes 6291456 | tf_op jit(solution)/shard_map/convert_element_type | solution.py:95
  141.7 72.0 %all_to_all.18 = bf16[2,512,1536]{2,0,1:T(2,128)(2,1)S(1)} all-to-all(bf16[2,512,1536]{2,0,1:T(2,128)(2,1)S(1)} %copy.100), channel_id=1, replica_groups=mesh['rep'=2,'span'=2,'seq'=4,'tp'=2] {'seq'}, dimensions={1} | all-to-all | bytes 6291456 | tf_op jit(solution)/shard_map/all_to_all | solution.py:94
  213.7 2.2 copy.101
  215.9 4.6 %copy.102 = bf16[2,128,4,1536]{1,3,2,0:T(8,128)(2,1)} copy(bf16[2,128,4,1536]{3,1,2,0:T(8,128)(2,1)} %bitcast.359) | data formatting | bytes 6291456 | tf_op jit(solution)/shard_map/all_to_all | solution.py:94
  221.6 48.3 %reduce-scatter.2.cloned.1.call-done = bf16[2,128,3072]{1,2,0:T(8,128)(2,1)} async-done(((bf16[2,128,6144]{1,2,0:T(8,128)(2,1)}), bf16[2,128,3072]{1,2,0:T(8,128)(2,1)}) %reduce-scatter.2.cloned.1.call-update) | async-done | bytes 1572880 | tf_op jit(solution)/shard_map/reduce_scatter | solution.py:97
  269.9 2.1 multiply_convert_fusion
  (53 shorter events, 30.1 us)
Async XLA Ops:
  6.5 214.7 %copy-start = (f32[64,3072]{1,0:T(8,128)S(1)}, f32[64,3072]{1,0:T(8,128)}, u32[]{:S(2)}) copy-start(f32[64,3072]{1,0:T(8,128)} %param.26) | copy-start | bytes 2359300
  6.5 37.2 %all-gather.3.cloned.1.call-start = ((), (), s32[]{:S(2)}) async-start(), calls=%async_computation.2 | async-start | bytes 1572864 | tf_op jit(solution)/shard_map/all_gather | solution.py:60
  25.6 27.7 %all-gather.5.cloned.1.call-start = ((), (), s32[]{:S(2)}) async-start(), calls=%async_computation.3 | async-start | bytes 1572864 | tf_op jit(solution)/shard_map/all_gather | solution.py:61
  43.6 226.3 %reduce-scatter.2.cloned.1.call-start = ((), (), s32[]{:S(2)}) async-start(), calls=%async_computation.4 | async-start | bytes 4718592 | tf_op jit(solution)/shard_map/reduce_scatter | solution.py:97
  78.7 13.8 %collective-permute-start = (bf16[2,128,1536]{2,1,0:T(8,128)(2,1)S(1)}, bf16[2,128,1536]{2,1,0:T(8,128)(2,1)S(1)}, u32[]{:S(2)}, u32[]{:S(2)}) collective-permute-start(bf16[2,128,1536]{2,1,0:T(8,128)(2,1)S(1)} %fusion.186), channel_id=1, source_target_pairs={{0,2},{2,4},{4,6},{6,0},{1,3},{3,5},{5,7},{7,1},{8,10},{10,12},{12... | collective-permute-start | bytes 2359304 | tf_op jit(solution)/shard_map/ppermute | solution.py:19
  92.5 13.9 %collective-permute-start.1 = (bf16[2,128,1536]{2,1,0:T(8,128)(2,1)S(1)}, bf16[2,128,1536]{2,1,0:T(8,128)(2,1)}, u32[]{:S(2)}, u32[]{:S(2)}) collective-permute-start(bf16[2,128,1536]{2,1,0:T(8,128)(2,1)S(1)} %collective-permute-done), channel_id=1, source_target_pairs={{0,2},{2,4},{4,6},{6,0},{1,3},{3,5},{5,7},{7,1},{8,10},{10,12},{12... | collective-permute-start | bytes 2359304 | tf_op jit(solution)/shard_map/ppermute | solution.py:19
  92.5 17.6 %slice-start = ((s8[4718592]{0:T(1024)(128)(4,1)}), s8[4194304]{0:T(1024)(128)(4,1)S(1)}, s32[]{:S(2)}) async-start(s8[4718592]{0:T(1024)(128)(4,1)} %bitcast.367), calls=%async_computation.5 | async-start | bytes 8388608
  92.5 17.6 %slice-start.1 = ((s8[4718592]{0:T(1024)(128)(4,1)}), s8[524288]{0:T(1024)(128)(4,1)S(1)}, s32[]{:S(2)}) async-start(s8[4718592]{0:T(1024)(128)(4,1)} %bitcast.367), calls=%async_computation.6 | async-start | bytes 1048576
  106.4 22.3 %collective-permute-start.2 = (bf16[2,128,1536]{2,1,0:T(8,128)(2,1)}, bf16[2,128,1536]{2,1,0:T(8,128)(2,1)S(1)}, u32[]{:S(2)}, u32[]{:S(2)}) collective-permute-start(bf16[2,128,1536]{2,1,0:T(8,128)(2,1)} %collective-permute-done.1), channel_id=1, source_target_pairs={{0,2},{2,4},{4,6},{6,0},{1,3},{3,5},{5,7},{7,1},{8,10},{10,12},{12... | collective-permute-start | bytes 2359304 | tf_op jit(solution)/shard_map/ppermute | solution.py:19
  220.5 0.7 copy-start.5
Sparse Core Ops, SparseCore 0:
  25.7 10.8 all-gather.2
  43.7 9.5 all-gather.4
  220.6 49.2 reduce-scatter.1
